TPU v7x, 256 devices: a whole 4x4x8 slice. The times are simulated.
256 devices in a mesh: dp: 32 (over x, y, core), tensor: 8 (over z).
Axes of the slice: x: 4, y: 4, z: 8, core: 2. Of those that a mesh axis runs over, the one named last changes fastest.
Arguments:
- query: bfloat16 [512, 4096], P('dp', 'tensor'), may hold values from -8000 to 8000
- incoming_key: bfloat16 [512, 2048], P('dp', 'tensor'), may hold values from -4.5 to 4.5
- new_value: bfloat16 [512, 2048], P('dp', 'tensor'), may hold values from -4.5 to 4.5
- key_cache: bfloat16 [512, 256, 2048], P('dp', None, 'tensor'), may hold values from -4.5 to 4.5
- value_cache: bfloat16 [512, 256, 2048], P('dp', None, 'tensor'), may hold values from -4.5 to 4.5
- cache_len: int32 [512], P('dp'), may hold values from 2 to 256
- out_weight: bfloat16 [4096, 4608], P('tensor'), may hold values from -0.09375 to 0.09375
- residual: bfloat16 [512, 4608], P('dp'), may hold values from -6 to 6
- post_gain: float32 [4608], replicated, may hold values from 0.5 to 1.5
- final_gain: float32 [4608], replicated, may hold values from 0.5 to 1.5
- vocab_weight: bfloat16 [131072, 4608], P(('dp', 'tensor')), may hold values from -113 to 113
- sampled: int32 [512], P('dp'), may hold values from 0 to 131071
- stop_flag: int32 [512], P('dp'), may hold values from 0 to 1, as said below
Outputs:
- new_residual: bfloat16 [512, 4608], P('dp', 'tensor')
- token_logprob: float32 [512], P('dp')
- insert_rank: int32 [512], P('dp')
- released_slot_total: int32 [], replicated
Inputs may be any that keep to these rules, and one draw needn't show every extreme that they name: `stop_flag`: each aligned block of 16 slots holds 1 to 16 stops.
All inputs are finite; a program needn't handle non-finite values.
Results may differ from a plain program's by a relative error of at most 0.0038.
The roundings to bfloat16 on the way count: a program that leaves them out, or rounds other values in their place, can miss the bound.
Values may be sent and summed in bfloat16 or wider, within the bound.
No kernel may reach another device: no remote copies, remote signals or barrier semaphores. Data moves between devices by JAX's collectives and lax.ppermute only.
A program may use at most 64 MiB of HBM per device.

v0:
```python
import jax
import jax.numpy as jnp
from jax import lax
from jax.sharding import Mesh
from jax.sharding import PartitionSpec as P

D = 4608
HEADS = 32
KV_HEADS = 16
HEAD_DIM = 128
DP = ("dp_0", "dp_1", "dp_2")
DP_TENSOR = ("dp_0", "dp_1", "dp_2", "tensor")


def gathered_total(shard, axis):
    return lax.all_gather(shard, axis).sum(0)


def all_in_one(shard, axis):
    leaves = jax.tree.leaves(shard)
    sequence = sorted(range(len(leaves)), key=lambda k: -leaves[k].size)
    width = (1, *leaves[sequence[0]].shape)[-1]
    lines = [
        jnp.pad(leaves[k].reshape(-1), (0, -leaves[k].size % width)).reshape(-1, width)
        for k in sequence
    ]
    both, at, found = (lax.all_gather(jnp.concatenate(lines), axis), 0, {})
    for k, line in zip(sequence, lines):
        share = both[:, at : at + len(line)].reshape(len(both), -1)
        found[k] = share[:, : leaves[k].size].reshape(-1, *leaves[k].shape)
        at += len(line)
    numbers = iter(range(len(leaves)))
    return jax.tree.map(lambda _: found[next(numbers)], shard)


def combined_by_axis(shard, axes, combine):
    for axis in axes:
        pieces = all_in_one(shard, axis)
        shard = jax.tree.map(lambda part: part[0], pieces)
        for k in range(1, lax.axis_size(axis)):
            shard = combine(shard, jax.tree.map(lambda part: part[k], pieces))
    return shard


def attend_local(query, incoming_key, new_value, key_cache, value_cache, cache_len):
    slot_dev = query.shape[0]
    positions = key_cache.shape[1]
    kv_local = incoming_key.shape[1] // HEAD_DIM
    group = HEADS // KV_HEADS
    query_vector = query.reshape(slot_dev, kv_local, group, HEAD_DIM)
    keys = key_cache.reshape(slot_dev, positions, kv_local, HEAD_DIM)
    values = value_cache.reshape(slot_dev, positions, kv_local, HEAD_DIM)
    self_key = incoming_key.reshape(slot_dev, kv_local, HEAD_DIM)
    own_value = new_value.reshape(slot_dev, kv_local, HEAD_DIM).astype(jnp.float32)
    scores = (
        jnp.einsum("bkgd,bckd->bkgc", query_vector, keys, preferred_element_type=jnp.float32) / 12.0
    )
    self_entry = (
        jnp.einsum("qyxm,qym->qyx", query_vector, self_key, preferred_element_type=jnp.float32)
        / 12.0
    )
    valid = (
        jnp.arange(positions, dtype=jnp.int32)[None, None, None, :] < cache_len[:, None, None, None]
    )
    scores = jnp.where(valid, scores, -1e30)
    top = jnp.maximum(jnp.max(scores, axis=-1), self_entry)
    expo = jnp.where(valid, jnp.exp(scores - top[..., None]), 0.0)
    own_exp = jnp.exp(self_entry - top)
    total = jnp.sum(expo, axis=-1) + own_exp
    weight = (expo / total[..., None]).astype(jnp.bfloat16)
    own_weight = (own_exp / total).astype(jnp.bfloat16).astype(jnp.float32)
    attn = jnp.einsum("bkgc,bckd->bkgd", weight, values, preferred_element_type=jnp.float32)
    attn = attn + own_weight[..., None] * own_value[:, :, None, :]
    return attn.astype(jnp.bfloat16).reshape(slot_dev, kv_local * group * HEAD_DIM)


def collect_slots(hidden, sampled):
    return (
        lax.all_gather(hidden, DP, axis=0, tiled=True),
        lax.all_gather(sampled, DP, axis=0, tiled=True),
    )


def combine_stats(first, second):
    top = jnp.maximum(first[0], second[0])
    total = first[1] * jnp.exp(first[0] - top) + second[1] * jnp.exp(second[0] - top)
    return (top, total, first[2] + second[2], first[3] + second[3])


def on_device(
    query,
    incoming_key,
    new_value,
    key_cache,
    value_cache,
    cache_len,
    out_weight,
    residual,
    post_gain,
    final_gain,
    vocab_weight,
    sampled,
    stop_flag,
):
    slot_dev = query.shape[0]
    attn = attend_local(query, incoming_key, new_value, key_cache, value_cache, cache_len)
    partial_value = jnp.dot(attn, out_weight, preferred_element_type=jnp.float32)
    whole = gathered_total(partial_value, "tensor")
    post = whole * lax.rsqrt(jnp.mean(whole * whole, axis=1, keepdims=True) + 1e-06) * post_gain
    full_mix = (residual.astype(jnp.float32) + post).astype(jnp.bfloat16)
    mixed = full_mix.astype(jnp.float32)
    hidden = (
        mixed * lax.rsqrt(jnp.mean(mixed * mixed, axis=1, keepdims=True) + 1e-06) * final_gain
    ).astype(jnp.bfloat16)
    width = D // lax.axis_size("tensor")
    new_residual = lax.dynamic_slice_in_dim(full_mix, lax.axis_index("tensor") * width, width, 1)
    every, ids = collect_slots(hidden, sampled)
    logits = lax.dot_general(
        every, vocab_weight, (((1,), (1,)), ((), ())), preferred_element_type=jnp.float32
    )
    vocabulary_per_device = vocab_weight.shape[0]
    vocab_start = (
        lax.axis_index(DP) * lax.axis_size("tensor") + lax.axis_index("tensor")
    ) * vocabulary_per_device
    local_ids = ids - vocab_start
    hit = jnp.arange(vocabulary_per_device, dtype=jnp.int32)[None, :] == local_ids[:, None]
    picked_part = jnp.sum(jnp.where(hit, logits, 0.0), axis=1)
    row_max = jnp.max(logits, axis=1)
    freed = (stop_flag == 1).astype(jnp.int32)
    count = jnp.sum(freed)
    groups = lax.axis_size(DP)
    lane_ids = jnp.arange(groups, dtype=jnp.int32)
    first_core = (lax.axis_index("tensor") == 0).astype(jnp.float32)
    lanes = jnp.where(lane_ids == lax.axis_index(DP), count.astype(jnp.float32) * first_core, 0.0)
    local_sum = jnp.sum(jnp.exp(logits - row_max[:, None]), axis=1)
    top, expsum, picked, tallied_entries = combined_by_axis(
        (row_max, local_sum, picked_part, lanes), DP_TENSOR, combine_stats
    )
    before = jnp.sum(jnp.where(lane_ids < lax.axis_index(DP), tallied_entries, 0.0)).astype(
        jnp.int32
    )
    released_count = jnp.sum(tallied_entries).astype(jnp.int32)
    logprob_all = picked - (jnp.log(expsum) + top)
    token_logprob = lax.dynamic_slice_in_dim(
        logprob_all, lax.axis_index(DP) * slot_dev, slot_dev, 0
    )
    local_before = jnp.cumsum(freed) - freed + before
    insert_rank = jnp.where(freed == 1, local_before, -1)
    return (new_residual, token_logprob, insert_rank, released_count)


def solution(mesh):
    split = Mesh(
        mesh.devices.reshape(4, 4, 2, mesh.shape["tensor"]), ("dp_0", "dp_1", "dp_2", "tensor")
    )
    in_specs = (
        P(DP, "tensor"),
        P(DP, "tensor"),
        P(DP, "tensor"),
        P(DP, None, "tensor"),
        P(DP, None, "tensor"),
        P(DP),
        P("tensor", None),
        P(DP, None),
        P(),
        P(),
        P(DP_TENSOR, None),
        P(DP),
        P(DP),
    )
    out_specs = (P(DP, "tensor"), P(DP), P(DP), P())
    return jax.shard_map(
        on_device, mesh=split, in_specs=in_specs, out_specs=out_specs, check_vma=False
    )
```

profile of v0, /device:TPU:2, one launch (start us, length us, event | category | flops | bytes accessed | tf_op | source)
XLA Modules:
  0.0 184.3 jit_solution(2291557467032989353)
XLA Ops:
  7.2 0.0 copy-start
  7.2 0.0 copy-start.4
  7.2 0.0 all-gather.14.cloned.1.call-start
  7.2 0.9 reshape.784
  8.1 0.7 reshape.834
  8.8 0.7 iota_compare_fusion.1
  9.5 0.1 fusion.85
  9.7 0.0 copy-done
  9.7 0.7 fusion.83
  10.5 0.2 fusion.22
  10.7 0.0 copy-done.4
  10.8 2.0 %fusion.15 = bf16[16,2,2,128]{3,2,1,0:T(2,128)(2,1)S(1)} fusion(f32[16,2,2]{2,1,0:T(2,128)S(1)} %get-tuple-element.34, f32[16,2,128]{2,1,0:T(2,128)S(1)} %reshape.802, f32[16,2,2]{2,1,0:T(2,128)S(1)} %get-tuple-element.33, f32[16,2,2,256]{3,2,1,0:T(2,128)S(1)} %get-tuple-element.36, pred[16,256]{1,0:T(8,128)(4,1)S(1)} %iota_compare_fusion.1, ...), kind=kOutput, calls=%fused_computation.9 | convolution fusion | flops 4284416 | bytes 2200320 | tf_op jit(solution)/shard_map/bkgc,bckd->bkgd/dot_general | solution.py:72
  12.8 3.8 %fusion.86 = f32[16,4608]{1,0:T(8,128)} fusion(bf16[16,512]{1,0:T(8,128)(2,1)S(1)} %reshape.788, bf16[512,4608]{1,0:T(8,128)(2,1)} %param.19), kind=kOutput, calls=%fused_computation.160 | convolution fusion | flops 75497472 | bytes 5029888 | tf_op jit(solution)/shard_map/dot_general | solution.py:107
  16.6 0.0 copy-start.1
  16.6 0.0 copy-start.2
  16.6 0.0 copy-start.3
  16.6 0.0 all-gather.14.cloned.1.call-update
  16.6 0.0 copy-start.5
  16.7 0.0 copy-start.7
  16.7 0.0 copy-start.6
  16.7 0.0 all-gather.12.cloned.1.call-start
  16.7 44.2 %all-gather.14.cloned.1.call-done = f32[128,4608]{1,0:T(8,128)} async-done(((f32[16,4608]{1,0:T(8,128)}), f32[128,4608]{1,0:T(8,128)}) %all-gather.14.cloned.1.call-update) | async-done | bytes 2359312 | tf_op jit(solution)/shard_map/all_gather | solution.py:16
  60.9 1.8 reduce_sum.82
  62.8 0.2 multiply_reduce_fusion
  62.9 0.0 copy-done.1
  62.9 0.0 copy-done.2
  62.9 0.3 fusion.18
  63.2 0.0 copy-done.3
  63.2 0.8 fusion.20
  64.0 0.0 all-gather.12.cloned.1.call-update
  64.0 0.0 copy-done.5
  64.0 0.6 fusion.74
  65.4 0.1 copy.25
  65.5 0.1 reduce.1
  65.6 0.0 copy-done.7
  65.6 0.6 dynamic-slice
  66.9 0.0 copy-done.6
  66.9 0.2 dynamic-update-slice
  67.1 15.3 %all-reduce.4 = s32[512]{0:T(512)S(1)} all-reduce(s32[512]{0:T(512)S(1)} %dynamic-update-slice), channel_id=1, replica_groups=mesh['dp_0'=4,'dp_1'=4,'dp_2'=2,'tensor'=8] {'dp_0','dp_1','dp_2'}, use_global_device_ids=true, to_apply=%add.4 | all-reduce | flops 512 | bytes 4096
  82.5 0.7 constant_dynamic-slice_fusion
  83.1 31.1 %all-gather.12.cloned.1.call-done = bf16[512,4608]{1,0:T(8,128)(2,1)} async-done(((bf16[16,4608]{1,0:T(8,128)(2,1)}), bf16[512,4608]{1,0:T(8,128)(2,1)}) %all-gather.12.cloned.1.call-update) | async-done | bytes 4718608 | tf_op jit(solution)/shard_map/all_gather | solution.py:79
  114.2 5.9 %fusion.84 = (f32[512]{0:T(512)S(1)}, f32[512,512]{0,1:T(8,128)S(1)}) fusion(bf16[512,4608]{1,0:T(8,128)(2,1)} %all-gather.12.cloned.1.call-done, bf16[512,4608]{1,0:T(8,128)(2,1)} %param.23), kind=kOutput, calls=%fused_computation.158 | convolution fusion | flops 2416180736 | bytes 10487808 | tf_op jit(solution)/shard_map/dot_general | solution.py:118
  120.2 0.3 exponential_reduce_fusion
  120.5 11.9 %all-gather.5 = f32[4,4,512]{2,1,0:T(4,128)S(1)} all-gather(f32[1,4,512]{2,1,0:T(4,128)S(1)} %maximum_bitcast_fusion), channel_id=3, replica_groups=mesh['dp_0'=4,'dp_1'=4,'dp_2'=2,'tensor'=8] {'dp_0'}, dimensions={0}, use_global_device_ids=true | all-gather | bytes 40960 | tf_op jit(solution)/shard_map/all_gather | solution.py:27
  132.5 11.9 %all-gather.6 = f32[4,4,512]{2,1,0:T(4,128)S(1)} all-gather(f32[1,4,512]{2,1,0:T(4,128)S(1)} %maximum_bitcast_fusion.1), channel_id=4, replica_groups=mesh['dp_0'=4,'dp_1'=4,'dp_2'=2,'tensor'=8] {'dp_1'}, dimensions={0}, use_global_device_ids=true | all-gather | bytes 40960 | tf_op jit(solution)/shard_map/all_gather | solution.py:27
  144.6 1.8 all-gather.7
  146.5 26.0 %all-gather.8 = f32[8,4,512]{2,1,0:T(4,128)S(1)} all-gather(f32[1,4,512]{2,1,0:T(4,128)S(1)} %maximum_bitcast_fusion.3), channel_id=6, replica_groups=mesh['dp_0'=4,'dp_1'=4,'dp_2'=2,'tensor'=8] {'tensor'}, dimensions={0}, use_global_device_ids=true | all-gather | bytes 73728 | tf_op jit(solution)/shard_map/all_gather | solution.py:27
  172.6 0.6 fusion.77
  173.2 0.6 fusion.69
  175.2 0.6 dynamic_slice.7
  175.8 0.5 compare_select_fusion.1
  (39 shorter events, 0.5 us)
Async XLA Ops:
  7.2 2.5 %copy-start = (bf16[16,256,256]{2,1,0:T(8,128)(2,1)S(1)}, bf16[16,256,256]{2,1,0:T(8,128)(2,1)}, u32[]{:S(2)}) copy-start(bf16[16,256,256]{2,1,0:T(8,128)(2,1)} %param.16) | copy-start | bytes 6291460
  7.2 3.5 %copy-start.4 = (bf16[16,256]{1,0:T(8,128)(2,1)S(1)}, bf16[16,256]{1,0:T(8,128)(2,1)}, u32[]{:S(2)}) copy-start(bf16[16,256]{1,0:T(8,128)(2,1)} %param.15) | copy-start | bytes 24580
  7.2 53.7 %all-gather.14.cloned.1.call-start = ((), (), s32[]{:S(2)}) async-start(), calls=%async_computation.1 | async-start | bytes 2654208 | tf_op jit(solution)/shard_map/all_gather | solution.py:16
  16.6 46.3 %copy-start.1 = (bf16[16,4608]{1,0:T(8,128)(2,1)S(1)}, bf16[16,4608]{1,0:T(8,128)(2,1)}, u32[]{:S(2)}) copy-start(bf16[16,4608]{1,0:T(8,128)(2,1)} %param.20) | copy-start | bytes 442372
  16.6 46.3 %copy-start.2 = (f32[4608]{0:T(1024)S(1)}, f32[4608]{0:T(1024)}, u32[]{:S(2)}) copy-start(f32[4608]{0:T(1024)} %param.21) | copy-start | bytes 55300
  16.6 46.6 %copy-start.3 = (f32[4608]{0:T(1024)S(1)}, f32[4608]{0:T(1024)}, u32[]{:S(2)}) copy-start(f32[4608]{0:T(1024)} %param.22) | copy-start | bytes 55300
  16.6 47.4 %copy-start.5 = (s32[16]{0:T(128)S(1)}, s32[16]{0:T(128)}, u32[]{:S(2)}) copy-start(s32[16]{0:T(128)} %param.25) | copy-start | bytes 196
  16.7 49.0 %copy-start.7 = (u32[256]{0:T(256)S(1)}, u32[256]{0:T(256)}, u32[]{:S(2)}) copy-start(u32[256]{0:T(256)} %constant.77) | copy-start | bytes 3076
  16.7 50.2 %copy-start.6 = (s32[16]{0:T(128)S(1)}, s32[16]{0:T(128)}, u32[]{:S(2)}) copy-start(s32[16]{0:T(128)} %param.24) | copy-start | bytes 196
  16.7 97.6 %all-gather.12.cloned.1.call-start = ((), (), s32[]{:S(2)}) async-start(), calls=%async_computation | async-start | bytes 4866048 | tf_op jit(solution)/shard_map/all_gather | solution.py:79
Sparse Core Ops, SparseCore 0:
  16.8 44.1 all-gather.13
  64.1 50.0 all-gather.11
where the time goes:
time: 185 us; the launch traced here: 184 us
  waiting for transfers between devices  75.3 us (41%)
  blocking collectives  67 us (36%)
  between operations  18.2 us (10%)
  matrix products  12.6 us (7%)
  other arithmetic  7.08 us (4%)
  local copies, waits for them, and re-layouts  3.94 us (2%)
    all_gather x4, blocking collectives, all_in_one(): both, at, found = (lax.all_gather(jnp.concatenate(lines), axis), 0, {})  51.7 us
    all_gather x1, waiting for transfers between devices, gathered_total(): return lax.all_gather(shard, axis).sum(0)  44.2 us
    all_gather x1, waiting for transfers between devices, collect_slots(): lax.all_gather(hidden, DP, axis=0, tiled=True)  31.1 us
    unnamed x1, blocking collectives  15.3 us
    dot_general x1, matrix products, on_device(): lax.dot_general(every, vocab_weight, (((1,), (1,)), ((), ())), preferred_...  5.93 us
    dot_general x1, matrix products, on_device(): jnp.dot(attn, out_weight, preferred_element_type=jnp.float32)  3.79 us
  transfers between devices with their start and end apart: 2, of which 2 were waited for; matrix products, arithmetic and copies ran while one was open for 1% of the time, Pallas kernels for 0%

commit v1 on v0

--- a/solution.py
+++ b/solution.py
@@ -10,6 +10,13 @@
 HEAD_DIM = 128
 DP = ("dp_0", "dp_1", "dp_2")
 DP_TENSOR = ("dp_0", "dp_1", "dp_2", "tensor")
+
+
+def connect_panels(body):
+    return jnp.concatenate(
+        jax.lax.all_to_all(jnp.stack([body for _ in range(jax.lax.axis_size(DP))]), DP, 0, 0),
+        axis=0,
+    )
 
 
 def gathered_total(shard, axis):
@@ -75,10 +82,7 @@
 
 
 def collect_slots(hidden, sampled):
-    return (
-        lax.all_gather(hidden, DP, axis=0, tiled=True),
-        lax.all_gather(sampled, DP, axis=0, tiled=True),
-    )
+    return (connect_panels(hidden), lax.all_gather(sampled, DP, axis=0, tiled=True))
 
 
 def combine_stats(first, second):

time: 185 us -> 208 us (1.12)
  blocking collectives: 67 us -> 110 us
  waiting for transfers between devices: 75.3 us -> 44.3 us
  starting transfers between devices: 0.08 us -> 7.63 us
  local copies, waits for them, and re-layouts: 3.94 us -> 6.63 us
    unnamed x1, blocking collectives: 15.3 us -> 60.9 us
    all_gather x1 -> x0, waiting for transfers between devices: 31.1 us -> none  [collect_slots(): lax.all_gather(hidden, DP, axis=0, tiled=True)]
    all_to_all x0 -> x1, starting transfers between devices: none -> 7.6 us  [connect_panels(): jax.lax.all_to_all(jnp.stack([body for _ in range(jax.lax.axis_size(DP))]...]
    another operation x1 -> x2, local copies, waits for them, and re-layouts: 0.08 us -> 2.78 us  [the longest x1 2.7 us: connect_panels(): jnp.stack([body for _ in range(jax.lax.axis_size(DP))])]
    all_gather x4, blocking collectives: 51.7 us -> 49.1 us  [all_in_one(): both, at, found = (lax.all_gather(jnp.concatenate(lines), axis), 0, {})]
  transfers between devices with their start and end apart: 2 -> 2, of which waited for: 2 -> 1; matrix products, arithmetic and copies ran while one was open for 1% -> 1% of each run, Pallas kernels for 0% -> 0%
where the time goes in v1:
time: 208 us; the launch traced here: 206 us
  blocking collectives  110 us (53%)
  waiting for transfers between devices  44.3 us (21%)
  between operations  18.1 us (9%)
  matrix products  12.6 us (6%)
  starting transfers between devices  7.63 us (4%)
  local copies, waits for them, and re-layouts  6.63 us (3%)
  other arithmetic  6.4 us (3%)
    unnamed x1, blocking collectives  60.9 us
    all_gather x4, blocking collectives, all_in_one(): both, at, found = (lax.all_gather(jnp.concatenate(lines), axis), 0, {})  49.1 us
    all_gather x1, waiting for transfers between devices, gathered_total(): return lax.all_gather(shard, axis).sum(0)  44.3 us
    all_to_all x1, starting transfers between devices, connect_panels(): jax.lax.all_to_all(jnp.stack([body for _ in range(jax.lax.axis_size(DP))]...  7.6 us
    dot_general x1, matrix products, on_device(): lax.dot_general(every, vocab_weight, (((1,), (1,)), ((), ())), preferred_...  5.93 us
  transfers between devices with their start and end apart: 2, of which 1 were waited for; matrix products, arithmetic and copies ran while one was open for 1% of the time, Pallas kernels for 0%

profile of v1, /device:TPU:2, one launch (start us, length us, event | category | flops | bytes accessed | tf_op | source)
XLA Modules:
  0.0 205.7 jit_solution(15334490493847468482)
XLA Ops:
  7.2 0.0 copy-start
  7.2 0.0 copy-start.4
  7.2 0.0 all-gather.11.cloned.1.call-start
  7.2 0.9 reshape.789
  8.1 0.7 reshape.840
  8.8 0.7 iota_compare_fusion.1
  9.5 0.1 fusion.85
  9.7 0.0 copy-done
  9.7 0.7 fusion.83
  10.5 0.2 fusion.22
  10.7 0.0 copy-done.4
  10.8 2.0 fusion.15
  12.8 3.8 %fusion.86 = f32[16,4608]{1,0:T(8,128)} fusion(bf16[16,512]{1,0:T(8,128)(2,1)S(1)} %reshape.793, bf16[512,4608]{1,0:T(8,128)(2,1)} %param.19), kind=kOutput, calls=%fused_computation.160 | convolution fusion | flops 75497472 | bytes 5029888 | tf_op jit(solution)/shard_map/dot_general | solution.py:111
  16.6 0.0 copy-start.1
  16.6 0.0 copy-start.2
  16.6 0.0 copy-start.3
  16.6 0.0 all-gather.11.cloned.1.call-update
  16.6 44.3 %all-gather.11.cloned.1.call-done = f32[128,4608]{1,0:T(8,128)} async-done(((f32[16,4608]{1,0:T(8,128)}), f32[128,4608]{1,0:T(8,128)}) %all-gather.11.cloned.1.call-update) | async-done | bytes 2359312 | tf_op jit(solution)/shard_map/all_gather | solution.py:23
  60.9 1.8 reduce_sum.82
  62.8 0.2 multiply_reduce_fusion
  62.9 0.0 copy-done.1
  62.9 0.0 copy-done.2
  62.9 0.3 fusion.18
  63.2 0.0 copy-done.3
  63.2 0.1 fusion.20
  63.3 2.7 %stack.2 = bf16[32,16,4608]{2,1,0:T(8,128)(2,1)} broadcast(bf16[16,4608]{1,0:T(8,128)(2,1)S(1)} %fusion.20), dimensions={1,2} | broadcast | bytes 4866048 | tf_op jit(solution)/shard_map/stack | solution.py:17
  66.0 0.0 copy-start.5
  66.0 0.0 copy-start.7
  66.0 0.0 copy-start.6
  66.0 7.6 %all-to-all-start = ((bf16[32,16,4608]{2,1,0:T(8,128)(2,1)}), bf16[32,16,4608]{2,1,0:T(8,128)(2,1)}, u32[]{:S(2)}, u32[]{:S(2)}) async-start(bf16[32,16,4608]{2,1,0:T(8,128)(2,1)} %stack.2), calls=%async_computation | async-start | bytes 9437184 | tf_op jit(solution)/shard_map/all_to_all | solution.py:17
  73.6 0.0 copy-done.5
  73.6 0.6 fusion.74
  75.0 0.1 copy.25
  75.1 0.1 reduce.1
  75.2 0.0 copy-done.7
  75.2 0.6 dynamic-slice
  76.5 0.0 copy-done.6
  76.5 0.2 dynamic-update-slice
  76.7 60.9 %all-reduce.4 = s32[512]{0:T(512)S(1)} all-reduce(s32[512]{0:T(512)S(1)} %dynamic-update-slice), channel_id=1, replica_groups=mesh['dp_0'=4,'dp_1'=4,'dp_2'=2,'tensor'=8] {'dp_0','dp_1','dp_2'}, use_global_device_ids=true, to_apply=%add.4 | all-reduce | flops 512 | bytes 4096
  137.6 0.7 constant_dynamic-slice_fusion
  138.3 0.0 all-to-all-done
  138.3 5.9 %fusion.84 = (f32[512]{0:T(512)S(1)}, f32[512,512]{0,1:T(8,128)S(1)}) fusion(bf16[512,4608]{1,0:T(8,128)(2,1)} %bitcast.3, bf16[512,4608]{1,0:T(8,128)(2,1)} %param.23), kind=kOutput, calls=%fused_computation.158 | convolution fusion | flops 2416180736 | bytes 10487808 | tf_op jit(solution)/shard_map/dot_general | solution.py:122
  144.2 0.3 exponential_reduce_fusion
  144.6 10.7 %all-gather.5 = f32[4,4,512]{2,1,0:T(4,128)S(1)} all-gather(f32[1,4,512]{2,1,0:T(4,128)S(1)} %maximum_bitcast_fusion), channel_id=3, replica_groups=mesh['dp_0'=4,'dp_1'=4,'dp_2'=2,'tensor'=8] {'dp_0'}, dimensions={0}, use_global_device_ids=true | all-gather | bytes 40960 | tf_op jit(solution)/shard_map/all_gather | solution.py:34
  155.4 11.9 %all-gather.6 = f32[4,4,512]{2,1,0:T(4,128)S(1)} all-gather(f32[1,4,512]{2,1,0:T(4,128)S(1)} %maximum_bitcast_fusion.1), channel_id=4, replica_groups=mesh['dp_0'=4,'dp_1'=4,'dp_2'=2,'tensor'=8] {'dp_1'}, dimensions={0}, use_global_device_ids=true | all-gather | bytes 40960 | tf_op jit(solution)/shard_map/all_gather | solution.py:34
  167.5 1.8 all-gather.7
  169.4 24.6 %all-gather.8 = f32[8,4,512]{2,1,0:T(4,128)S(1)} all-gather(f32[1,4,512]{2,1,0:T(4,128)S(1)} %maximum_bitcast_fusion.3), channel_id=6, replica_groups=mesh['dp_0'=4,'dp_1'=4,'dp_2'=2,'tensor'=8] {'tensor'}, dimensions={0}, use_global_device_ids=true | all-gather | bytes 73728 | tf_op jit(solution)/shard_map/all_gather | solution.py:34
  194.1 0.6 fusion.77
  194.7 0.6 fusion.69
  196.6 0.6 dynamic_slice.7
  197.2 0.5 compare_select_fusion.1
  (39 shorter events, 0.5 us)
Async XLA Ops:
  7.2 2.5 %copy-start = (bf16[16,256,256]{2,1,0:T(8,128)(2,1)S(1)}, bf16[16,256,256]{2,1,0:T(8,128)(2,1)}, u32[]{:S(2)}) copy-start(bf16[16,256,256]{2,1,0:T(8,128)(2,1)} %param.16) | copy-start | bytes 6291460
  7.2 3.5 %copy-start.4 = (bf16[16,256]{1,0:T(8,128)(2,1)S(1)}, bf16[16,256]{1,0:T(8,128)(2,1)}, u32[]{:S(2)}) copy-start(bf16[16,256]{1,0:T(8,128)(2,1)} %param.15) | copy-start | bytes 24580
  7.2 53.8 %all-gather.11.cloned.1.call-start = ((), (), s32[]{:S(2)}) async-start(), calls=%async_computation.1 | async-start | bytes 2654208 | tf_op jit(solution)/shard_map/all_gather | solution.py:23
  16.6 46.3 %copy-start.1 = (bf16[16,4608]{1,0:T(8,128)(2,1)S(1)}, bf16[16,4608]{1,0:T(8,128)(2,1)}, u32[]{:S(2)}) copy-start(bf16[16,4608]{1,0:T(8,128)(2,1)} %param.20) | copy-start | bytes 442372
  16.6 46.3 %copy-start.2 = (f32[4608]{0:T(1024)S(1)}, f32[4608]{0:T(1024)}, u32[]{:S(2)}) copy-start(f32[4608]{0:T(1024)} %param.21) | copy-start | bytes 55300
  16.6 46.6 %copy-start.3 = (f32[4608]{0:T(1024)S(1)}, f32[4608]{0:T(1024)}, u32[]{:S(2)}) copy-start(f32[4608]{0:T(1024)} %param.22) | copy-start | bytes 55300
  66.0 7.6 %copy-start.5 = (s32[16]{0:T(128)S(1)}, s32[16]{0:T(128)}, u32[]{:S(2)}) copy-start(s32[16]{0:T(128)} %param.25) | copy-start | bytes 196
  66.0 9.2 %copy-start.7 = (u32[256]{0:T(256)S(1)}, u32[256]{0:T(256)}, u32[]{:S(2)}) copy-start(u32[256]{0:T(256)} %constant.77) | copy-start | bytes 3076
  66.0 10.5 %copy-start.6 = (s32[16]{0:T(128)S(1)}, s32[16]{0:T(128)}, u32[]{:S(2)}) copy-start(s32[16]{0:T(128)} %param.24) | copy-start | bytes 196
  66.0 72.3 %all-to-all-start = ((bf16[32,16,4608]{2,1,0:T(8,128)(2,1)}), bf16[32,16,4608]{2,1,0:T(8,128)(2,1)}, u32[]{:S(2)}, u32[]{:S(2)}) async-start(bf16[32,16,4608]{2,1,0:T(8,128)(2,1)} %stack.2), calls=%async_computation | async-start | bytes 9437184 | tf_op jit(solution)/shard_map/all_to_all | solution.py:17
Sparse Core Ops, SparseCore 0:
  16.8 44.1 all-gather.10
